TPU v7x, 32 devices: a whole 2x2x4 slice. The times are simulated.
32 devices in a mesh: img: 2 (over y), row: 8 (over z, x), col: 2 (over core).
Axes of the slice: x: 2, y: 2, z: 4, core: 2. Of those that a mesh axis runs over, the one named last changes fastest.
Arguments:
- features: bfloat16 [16, 128, 512], P(('img', 'row'), 'col'), parts along dimension 0, may hold values from -60 to 60
- first_gain: float32 [512], replicated, may hold values from 0.1 to 1.9
- first_shift: float32 [512], replicated, may hold values from -2.5 to 2.5
- first_weight: bfloat16 [3, 3, 512, 512], P(None, None, 'row'), may hold values from -0.09375 to 0.09375
- first_bias: float32 [512], replicated, may hold values from -2.5 to 2.5
- second_gain: float32 [512], replicated, may hold values from 0.1 to 1.9
- second_shift: float32 [512], replicated, may hold values from -2.5 to 2.5
- second_weight: bfloat16 [3, 3, 512, 512], P(None, None, 'row'), may hold values from -0.09375 to 0.09375
- second_bias: float32 [512], replicated, may hold values from -2.5 to 2.5
- upsample_weight: bfloat16 [3, 3, 512, 512], P(None, None, 'row'), may hold values from -0.09375 to 0.09375
- upsample_bias: float32 [512], replicated, may hold values from -2.5 to 2.5
Outputs:
- upsampled: bfloat16 [32, 256, 512], P(('img', 'row'), 'col'), parts along dimension 0
There are 2 independent parts, one for each index of `img`. A program takes and returns all parts, laid end to end along the dimension named above; an argument that names none is the same for every part. Nothing has to cross between parts.
All inputs are finite; a program needn't handle non-finite values.
Results may differ from a plain program's by a relative error of at most 0.0075.
Values may be sent and summed in bfloat16 or wider, within the bound.
A program may use at most 128 MiB of HBM per device.

v0:
```python
import jax
import jax.numpy as jnp
from jax import lax
from jax.sharding import PartitionSpec as P

G = 32
EPS = 1e-06


def extended(cells, sides, width):
    for axis, dim in sides:
        count = lax.axis_size(axis)
        ends = count - 1
        head = lax.slice_in_dim(cells, 0, width, axis=dim)
        tail = lax.slice_in_dim(cells, cells.shape[dim] - width, cells.shape[dim], axis=dim)
        cells = jnp.concatenate(
            [
                lax.ppermute(tail, axis, [(i, (i + 1) % count) for i in range(ends)]),
                cells,
                lax.ppermute(head, axis, [((i + 1) % count, i) for i in range(ends)]),
            ],
            axis=dim,
        )
    return cells


def norm_silu(values, gain, shift):
    height, breadth, channels = values.shape
    grouped = values.reshape(height * breadth, G, channels // G)
    total = jnp.sum(grouped, axis=(0, 2))
    squares = jnp.sum(grouped * grouped, axis=(0, 2))
    total, squares = lax.psum((total, squares), ("row", "col"))
    count = height * breadth * lax.axis_size("row") * lax.axis_size("col") * (channels // G)
    mean = total / count
    var = squares / count - mean * mean
    factor = lax.rsqrt(var + EPS)
    normed = (grouped - mean[None, :, None]) * factor[None, :, None]
    normed = normed.reshape(height, breadth, channels) * gain + shift
    return jax.nn.silu(normed).astype(jnp.bfloat16)


def extend(values):
    return extended(values, (("row", 0), ("col", 1)), 1)


def convolve(padded, weight, bias, height, breadth):
    outputs = weight.shape[3]
    empty = jnp.zeros((height, breadth, outputs), jnp.float32)
    share = weight.shape[2] // lax.axis_size("col")
    own = lax.dynamic_slice_in_dim(weight, lax.axis_index("col") * share, share, 2)
    total = empty
    piece = lax.all_gather(own, ("row", "col"), axis=2, tiled=True)
    depth = piece.shape[2]
    offset = jnp.asarray(jnp.int32(0), jnp.int32)
    for offset_y in range(3):
        for offset_x in range(3):
            window = lax.dynamic_slice(
                padded, (jnp.int32(offset_y), jnp.int32(offset_x), offset), (height, breadth, depth)
            )
            total = total + jnp.einsum(
                "hwk,kc->hwc", window, piece[offset_y, offset_x], preferred_element_type=jnp.float32
            )
    return total + bias


def on_device(
    features,
    first_gain,
    first_shift,
    first_weight,
    first_bias,
    second_gain,
    second_shift,
    second_weight,
    second_bias,
    upsample_weight,
    upsample_bias,
):
    height, breadth, channels = features.shape
    normed_one = norm_silu(features.astype(jnp.float32), first_gain, first_shift)
    hidden = convolve(extend(normed_one), first_weight, first_bias, height, breadth).astype(
        jnp.bfloat16
    )
    normed_two = norm_silu(hidden.astype(jnp.float32), second_gain, second_shift)
    block_out = (
        convolve(extend(normed_two), second_weight, second_bias, height, breadth)
        + features.astype(jnp.float32)
    ).astype(jnp.bfloat16)
    doubled = jnp.repeat(jnp.repeat(block_out, 2, axis=0), 2, axis=1)
    padded = extend(doubled)
    return convolve(padded, upsample_weight, upsample_bias, 2 * height, 2 * breadth).astype(
        jnp.bfloat16
    )


def solution(mesh):
    return jax.shard_map(
        on_device,
        mesh=mesh,
        in_specs=(
            P(("img", "row"), "col", None),
            P(),
            P(),
            P(None, None, "row", None),
            P(),
            P(),
            P(),
            P(None, None, "row", None),
            P(),
            P(None, None, "row", None),
            P(),
        ),
        out_specs=P(("img", "row"), "col", None),
        check_vma=False,
    )
```

profile of v0, /device:TPU:1, one launch (start us, length us, event | category | flops | bytes accessed | tf_op | source)
XLA Modules:
  0.0 196.7 jit_solution(13874195632810738690)
XLA Ops:
  8.4 1.7 constant_dynamic-slice_fusion.1
  10.2 1.7 constant_dynamic-slice_fusion
  13.2 31.1 %all-reduce.1 = (f32[32]{0:T(128)S(1)}, f32[32]{0:T(128)S(1)}) all-reduce(f32[32]{0:T(128)S(1)} %reduce_sum.54, f32[32]{0:T(128)S(1)} %reduce_sum.51), channel_id=1, replica_groups=mesh['img'=2,'row'=8,'col'=2] {'row','col'}, use_global_device_ids=true, to_apply=%region_5.6 | all-reduce | flops 64 | bytes 512 | tf_op jit(solution)/shard_map/psum | solution.py:32
  45.6 1.3 collective-permute-start
  46.9 1.3 collective-permute-start.1
  48.2 1.8 collective-permute-done
  50.0 3.9 %collective-permute-done.1 = bf16[1,64,512]{2,1,0:T(8,128)(2,1)S(1)} collective-permute-done((bf16[1,64,512]{2,1,0:T(8,128)(2,1)S(1)}, bf16[1,64,512]{2,1,0:T(8,128)(2,1)S(1)}, u32[]{:S(2)}, u32[]{:S(2)}) %collective-permute-start.1) | collective-permute-done | bytes 65568 | tf_op jit(solution)/shard_map/ppermute | solution.py:20
  53.9 1.3 collective-permute-start.2
  55.2 5.6 %collective-permute-start.3 = (bf16[3,1,512]{2,1,0:T(2,128)(2,1)S(1)}, bf16[3,1,512]{2,1,0:T(2,128)(2,1)S(1)}, u32[]{:S(2)}, u32[]{:S(2)}) collective-permute-start(bf16[3,1,512]{2,1,0:T(2,128)(2,1)S(1)} %get-tuple-element.20), channel_id=1, source_target_pairs={{1,0},{3,2},{5,4},{7,6},{9,8},{11,10},{13,12},{15,14},{17,16},{19,... | collective-permute-start | bytes 9224 | tf_op jit(solution)/shard_map/ppermute | solution.py:20
  60.7 7.4 %all-gather.4.cloned.1.call-done = bf16[3,3,512,512]{3,2,1,0:T(8,128)(2,1)} async-done(((bf16[3,3,32,512]{3,2,1,0:T(8,128)(2,1)}), bf16[3,3,512,512]{3,2,1,0:T(8,128)(2,1)}) %all-gather.4.cloned.1.call-update) | async-done | bytes 4718608 | tf_op jit(solution)/shard_map/all_gather | solution.py:52
  78.2 1.3 fusion.151
  79.9 30.2 %all-reduce = (f32[32]{0:T(128)S(1)}, f32[32]{0:T(128)S(1)}) all-reduce(f32[32]{0:T(128)S(1)} %reduce_sum.75, f32[32]{0:T(128)S(1)} %reduce_sum.72), channel_id=1, replica_groups=mesh['img'=2,'row'=8,'col'=2] {'row','col'}, use_global_device_ids=true, to_apply=%region_11.12 | all-reduce | flops 64 | bytes 512 | tf_op jit(solution)/shard_map/psum | solution.py:32
  110.5 1.3 collective-permute-start.4
  111.8 1.3 collective-permute-start.5
  113.1 10.3 %all-gather.6.cloned.1.call-done = bf16[3,3,512,512]{3,2,1,0:T(8,128)(2,1)} async-done(((bf16[3,3,32,512]{3,2,1,0:T(8,128)(2,1)}), bf16[3,3,512,512]{3,2,1,0:T(8,128)(2,1)}) %all-gather.6.cloned.1.call-update) | async-done | bytes 4718608 | tf_op jit(solution)/shard_map/all_gather | solution.py:52
  124.7 2.2 %collective-permute-start.7 = (bf16[3,1,512]{2,1,0:T(2,128)(2,1)S(1)}, bf16[3,1,512]{2,1,0:T(2,128)(2,1)S(1)}, u32[]{:S(2)}, u32[]{:S(2)}) collective-permute-start(bf16[3,1,512]{2,1,0:T(2,128)(2,1)S(1)} %get-tuple-element.18), channel_id=1, source_target_pairs={{1,0},{3,2},{5,4},{7,6},{9,8},{11,10},{13,12},{15,14},{17,16},{19,... | collective-permute-start | bytes 9224 | tf_op jit(solution)/shard_map/ppermute | solution.py:20
  126.9 1.3 collective-permute-start.6
  138.5 2.4 %collective-permute-start.8 = (bf16[1,128,512]{2,1,0:T(8,128)(2,1)S(1)}, bf16[1,128,512]{2,1,0:T(8,128)(2,1)S(1)}, u32[]{:S(2)}, u32[]{:S(2)}) collective-permute-start(bf16[1,128,512]{2,1,0:T(8,128)(2,1)S(1)} %slice.150), channel_id=1, source_target_pairs={{0,2},{2,4},{4,6},{6,8},{8,10},{10,12},{12,14},{1,3},{3,5},{5,7},{... | collective-permute-start | bytes 393224 | tf_op jit(solution)/shard_map/ppermute | solution.py:18
  140.9 1.3 collective-permute-start.9
  142.2 36.5 %all-gather.8.cloned.1.call-done = bf16[3,3,512,512]{3,2,1,0:T(8,128)(2,1)} async-done(((bf16[3,3,32,512]{3,2,1,0:T(8,128)(2,1)}), bf16[3,3,512,512]{3,2,1,0:T(8,128)(2,1)}) %all-gather.8.cloned.1.call-update) | async-done | bytes 4718608 | tf_op jit(solution)/shard_map/all_gather | solution.py:52
  178.8 1.5 fusion.31
  181.6 3.0 %collective-permute-start.11 = (bf16[4,1,512]{2,1,0:T(2,128)(2,1)S(1)}, bf16[4,1,512]{2,1,0:T(2,128)(2,1)S(1)}, u32[]{:S(2)}, u32[]{:S(2)}) collective-permute-start(bf16[4,1,512]{2,1,0:T(2,128)(2,1)S(1)} %get-tuple-element.16), channel_id=1, source_target_pairs={{1,0},{3,2},{5,4},{7,6},{9,8},{11,10},{13,12},{15,14},{17,16},{19,... | collective-permute-start | bytes 12296 | tf_op jit(solution)/shard_map/ppermute | solution.py:20
  184.7 1.3 fusion.34
  186.0 1.3 fusion.29
  (86 shorter events, 30.9 us)
Async XLA Ops:
  6.5 1.1 copy-start
  6.5 61.6 %all-gather.4.cloned.1.call-start = ((), (), s32[]{:S(2)}) async-start(), calls=%async_computation | async-start | bytes 5013504 | tf_op jit(solution)/shard_map/all_gather | solution.py:52
  8.4 69.8 %copy-start.3 = (f32[512]{0:T(512)S(1)}, f32[512]{0:T(512)}, u32[]{:S(2)}) copy-start(f32[512]{0:T(512)} %param.15) | copy-start | bytes 6148
  8.4 115.0 %all-gather.6.cloned.1.call-start = ((), (), s32[]{:S(2)}) async-start(), calls=%async_computation.1 | async-start | bytes 5013504 | tf_op jit(solution)/shard_map/all_gather | solution.py:52
  10.2 168.6 %all-gather.8.cloned.1.call-start = ((), (), s32[]{:S(2)}) async-start(), calls=%async_computation.2 | async-start | bytes 5013504 | tf_op jit(solution)/shard_map/all_gather | solution.py:52
  11.9 98.5 %copy-start.4 = (f32[512]{0:T(512)S(1)}, f32[512]{0:T(512)}, u32[]{:S(2)}) copy-start(f32[512]{0:T(512)} %param.17) | copy-start | bytes 6148
  11.9 98.5 %copy-start.5 = (f32[512]{0:T(512)S(1)}, f32[512]{0:T(512)}, u32[]{:S(2)}) copy-start(f32[512]{0:T(512)} %param.16) | copy-start | bytes 6148
  45.6 4.4 %collective-permute-start = (bf16[1,64,512]{2,1,0:T(8,128)(2,1)S(1)}, bf16[1,64,512]{2,1,0:T(8,128)(2,1)S(1)}, u32[]{:S(2)}, u32[]{:S(2)}) collective-permute-start(bf16[1,64,512]{2,1,0:T(8,128)(2,1)S(1)} %fusion.69), channel_id=1, source_target_pairs={{0,2},{2,4},{4,6},{6,8},{8,10},{10,12},{12,14},{1,3},{3,5},{5,7},{... | collective-permute-start | bytes 196616 | tf_op jit(solution)/shard_map/ppermute | solution.py:18
  46.9 6.9 %collective-permute-start.1 = (bf16[1,64,512]{2,1,0:T(8,128)(2,1)S(1)}, bf16[1,64,512]{2,1,0:T(8,128)(2,1)S(1)}, u32[]{:S(2)}, u32[]{:S(2)}) collective-permute-start(bf16[1,64,512]{2,1,0:T(8,128)(2,1)S(1)} %fusion.69), channel_id=1, source_target_pairs={{2,0},{4,2},{6,4},{8,6},{10,8},{12,10},{14,12},{3,1},{5,3},{7,5},{... | collective-permute-start | bytes 196616 | tf_op jit(solution)/shard_map/ppermute | solution.py:20
  53.9 6.9 %collective-permute-start.2 = (bf16[3,1,512]{2,1,0:T(2,128)(2,1)S(1)}, bf16[3,1,512]{2,1,0:T(2,128)(2,1)S(1)}, u32[]{:S(2)}, u32[]{:S(2)}) collective-permute-start(bf16[3,1,512]{2,1,0:T(2,128)(2,1)S(1)} %get-tuple-element.19), channel_id=1, source_target_pairs={{0,1},{2,3},{4,5},{6,7},{8,9},{10,11},{12,13},{14,15},{16,17},{18,... | collective-permute-start | bytes 9224 | tf_op jit(solution)/shard_map/ppermute | solution.py:18
  55.2 15.4 %collective-permute-start.3 = (bf16[3,1,512]{2,1,0:T(2,128)(2,1)S(1)}, bf16[3,1,512]{2,1,0:T(2,128)(2,1)S(1)}, u32[]{:S(2)}, u32[]{:S(2)}) collective-permute-start(bf16[3,1,512]{2,1,0:T(2,128)(2,1)S(1)} %get-tuple-element.20), channel_id=1, source_target_pairs={{1,0},{3,2},{5,4},{7,6},{9,8},{11,10},{13,12},{15,14},{17,16},{19,... | collective-permute-start | bytes 9224 | tf_op jit(solution)/shard_map/ppermute | solution.py:20
  78.2 58.8 %copy-start.2 = (bf16[1,64,512]{2,1,0:T(8,128)(2,1)S(1)}, bf16[1,64,512]{2,1,0:T(8,128)(2,1)}, u32[]{:S(2)}) copy-start(bf16[1,64,512]{2,1,0:T(8,128)(2,1)} %param.11) | copy-start | bytes 196612
  78.2 58.8 %copy-start.6 = (f32[512]{0:T(512)S(1)}, f32[512]{0:T(512)}, u32[]{:S(2)}) copy-start(f32[512]{0:T(512)} %param.19) | copy-start | bytes 6148
  110.5 14.2 %collective-permute-start.4 = (bf16[1,64,512]{2,1,0:T(8,128)(2,1)S(1)}, bf16[1,64,512]{2,1,0:T(8,128)(2,1)S(1)}, u32[]{:S(2)}, u32[]{:S(2)}) collective-permute-start(bf16[1,64,512]{2,1,0:T(8,128)(2,1)S(1)} %fusion.153), channel_id=1, source_target_pairs={{0,2},{2,4},{4,6},{6,8},{8,10},{10,12},{12,14},{1,3},{3,5},{5,7},{... | collective-permute-start | bytes 196616 | tf_op jit(solution)/shard_map/ppermute | solution.py:18
  111.8 12.9 %collective-permute-start.5 = (bf16[1,64,512]{2,1,0:T(8,128)(2,1)S(1)}, bf16[1,64,512]{2,1,0:T(8,128)(2,1)S(1)}, u32[]{:S(2)}, u32[]{:S(2)}) collective-permute-start(bf16[1,64,512]{2,1,0:T(8,128)(2,1)S(1)} %fusion.153), channel_id=1, source_target_pairs={{2,0},{4,2},{6,4},{8,6},{10,8},{12,10},{14,12},{3,1},{5,3},{7,5},{... | collective-permute-start | bytes 196616 | tf_op jit(solution)/shard_map/ppermute | solution.py:20
  124.7 8.5 %collective-permute-start.7 = (bf16[3,1,512]{2,1,0:T(2,128)(2,1)S(1)}, bf16[3,1,512]{2,1,0:T(2,128)(2,1)S(1)}, u32[]{:S(2)}, u32[]{:S(2)}) collective-permute-start(bf16[3,1,512]{2,1,0:T(2,128)(2,1)S(1)} %get-tuple-element.18), channel_id=1, source_target_pairs={{1,0},{3,2},{5,4},{7,6},{9,8},{11,10},{13,12},{15,14},{17,16},{19,... | collective-permute-start | bytes 9224 | tf_op jit(solution)/shard_map/ppermute | solution.py:20
  126.9 3.8 %collective-permute-start.6 = (bf16[3,1,512]{2,1,0:T(2,128)(2,1)S(1)}, bf16[3,1,512]{2,1,0:T(2,128)(2,1)S(1)}, u32[]{:S(2)}, u32[]{:S(2)}) collective-permute-start(bf16[3,1,512]{2,1,0:T(2,128)(2,1)S(1)} %get-tuple-element.17), channel_id=1, source_target_pairs={{0,1},{2,3},{4,5},{6,7},{8,9},{10,11},{12,13},{14,15},{16,17},{18,... | collective-permute-start | bytes 9224 | tf_op jit(solution)/shard_map/ppermute | solution.py:18
  138.5 41.7 %collective-permute-start.8 = (bf16[1,128,512]{2,1,0:T(8,128)(2,1)S(1)}, bf16[1,128,512]{2,1,0:T(8,128)(2,1)S(1)}, u32[]{:S(2)}, u32[]{:S(2)}) collective-permute-start(bf16[1,128,512]{2,1,0:T(8,128)(2,1)S(1)} %slice.150), channel_id=1, source_target_pairs={{0,2},{2,4},{4,6},{6,8},{8,10},{10,12},{12,14},{1,3},{3,5},{5,7},{... | collective-permute-start | bytes 393224 | tf_op jit(solution)/shard_map/ppermute | solution.py:18
  140.9 39.3 %collective-permute-start.9 = (bf16[1,128,512]{2,1,0:T(8,128)(2,1)S(1)}, bf16[1,128,512]{2,1,0:T(8,128)(2,1)S(1)}, u32[]{:S(2)}, u32[]{:S(2)}) collective-permute-start(bf16[1,128,512]{2,1,0:T(8,128)(2,1)S(1)} %slice.150), channel_id=1, source_target_pairs={{2,0},{4,2},{6,4},{8,6},{10,8},{12,10},{14,12},{3,1},{5,3},{7,5},{... | collective-permute-start | bytes 393224 | tf_op jit(solution)/shard_map/ppermute | solution.py:20
  178.8 8.8 %copy-start.1 = (bf16[3,3,512,512]{3,2,1,0:T(8,128)(2,1)S(1)}, bf16[3,3,512,512]{3,2,1,0:T(8,128)(2,1)}, u32[]{:S(2)}) copy-start(bf16[3,3,512,512]{3,2,1,0:T(8,128)(2,1)} %all-gather.8.cloned.1.call-done) | copy-start | bytes 14155780
  180.3 7.0 %collective-permute-start.10 = (bf16[4,1,512]{2,1,0:T(2,128)(2,1)S(1)}, bf16[4,1,512]{2,1,0:T(2,128)(2,1)S(1)}, u32[]{:S(2)}, u32[]{:S(2)}) collective-permute-start(bf16[4,1,512]{2,1,0:T(2,128)(2,1)S(1)} %get-tuple-element.15), channel_id=1, source_target_pairs={{0,1},{2,3},{4,5},{6,7},{8,9},{10,11},{12,13},{14,15},{16,17},{18,... | collective-permute-start | bytes 12296 | tf_op jit(solution)/shard_map/ppermute | solution.py:18
  181.6 5.7 %collective-permute-start.11 = (bf16[4,1,512]{2,1,0:T(2,128)(2,1)S(1)}, bf16[4,1,512]{2,1,0:T(2,128)(2,1)S(1)}, u32[]{:S(2)}, u32[]{:S(2)}) collective-permute-start(bf16[4,1,512]{2,1,0:T(2,128)(2,1)S(1)} %get-tuple-element.16), channel_id=1, source_target_pairs={{1,0},{3,2},{5,4},{7,6},{9,8},{11,10},{13,12},{15,14},{17,16},{19,... | collective-permute-start | bytes 12296 | tf_op jit(solution)/shard_map/ppermute | solution.py:20
  187.5 1.6 copy-start.7
Sparse Core Ops, SparseCore 0:
  9.5 58.5 all-gather.3
  70.3 53.0 all-gather.5
  125.6 53.0 all-gather.7
where the time goes:
time: 198 us; the launch traced here: 197 us
  blocking collectives  61.3 us (31%)
  waiting for transfers between devices  59.9 us (30%)
  matrix products  29.3 us (15%)
  starting transfers between devices  23.6 us (12%)
  between operations  13.6 us (7%)
  local copies, waits for them, and re-layouts  6.39 us (3%)
  other arithmetic  2.58 us (1%)
    psum x2, blocking collectives, norm_silu(): total, squares = lax.psum((total, squares), ('row', 'col'))  61.3 us
    all_gather x3, waiting for transfers between devices, convolve(): piece = lax.all_gather(own, ('row', 'col'), axis=2, tiled=True)  54.2 us
    dot_general x27, matrix products, convolve(): jnp.einsum('hwk,kc->hwc', window, piece[offset_y, offset_x], preferred_el...  29.3 us
    ppermute x6, starting transfers between devices, extended(): lax.ppermute(head, axis, [((i + 1) % count, i) for i in range(ends)])  14.6 us
    ppermute x6, starting transfers between devices, extended(): lax.ppermute(tail, axis, [(i, (i + 1) % count) for i in range(ends)])  8.86 us
    dynamic_slice x3, local copies, waits for them, and re-layouts, convolve(): lax.dynamic_slice_in_dim(weight, lax.axis_index('col') * share, share, 2)  4.17 us
  transfers between devices with their start and end apart: 15, of which 5 were waited for; matrix products, arithmetic and copies ran while one was open for 17% of the time, Pallas kernels for 0%

commit v1 on v0

--- a/solution.py
+++ b/solution.py
@@ -49,7 +49,7 @@
     share = weight.shape[2] // lax.axis_size("col")
     own = lax.dynamic_slice_in_dim(weight, lax.axis_index("col") * share, share, 2)
     total = empty
-    piece = lax.all_gather(own, ("row", "col"), axis=2, tiled=True)
+    piece = jnp.concatenate(lax.all_gather(own, ("row", "col")), axis=2)
     depth = piece.shape[2]
     offset = jnp.asarray(jnp.int32(0), jnp.int32)
     for offset_y in range(3):

time: 198 us -> 220 us (1.11)
  waiting for transfers between devices: 59.9 us -> 87.2 us
  matrix products: 29.3 us -> 11.5 us
  local copies, waits for them, and re-layouts: 6.39 us -> 19.5 us
    all_gather x3, waiting for transfers between devices: 54.2 us -> 75.5 us  [convolve(): piece = jnp.concatenate(lax.all_gather(own, ('row', 'col')), axis=2)]
    dot_general x27, matrix products: 29.3 us -> 11.5 us  [convolve(): jnp.einsum('hwk,kc->hwc', window, piece[offset_y, offset_x], preferred_el...]
    reshape x0 -> x2, local copies, waits for them, and re-layouts: none -> 5.47 us  [convolve(): piece = jnp.concatenate(lax.all_gather(own, ('row', 'col')), axis=2)]
    all_gather x0 -> x1, local copies, waits for them, and re-layouts: none -> 5.42 us  [convolve(): piece = jnp.concatenate(lax.all_gather(own, ('row', 'col')), axis=2)]
    ppermute x6, waiting for transfers between devices: 3.89 us -> 8.53 us  [extended(): lax.ppermute(head, axis, [((i + 1) % count, i) for i in range(ends)])]
  transfers between devices with their start and end apart: 15 -> 15, of which waited for: 5 -> 7; matrix products, arithmetic and copies ran while one was open for 17% -> 11% of each run, Pallas kernels for 0% -> 0%
where the time goes in v1:
time: 220 us; the launch traced here: 219 us
  waiting for transfers between devices  87.2 us (40%)
  blocking collectives  60.9 us (28%)
  starting transfers between devices  23.3 us (11%)
  local copies, waits for them, and re-layouts  19.5 us (9%)
  between operations  13.7 us (6%)
  matrix products  11.5 us (5%)
  other arithmetic  2.58 us (1%)
    all_gather x3, waiting for transfers between devices, convolve(): piece = jnp.concatenate(lax.all_gather(own, ('row', 'col')), axis=2)  75.5 us
    psum x2, blocking collectives, norm_silu(): total, squares = lax.psum((total, squares), ('row', 'col'))  60.9 us
    ppermute x6, starting transfers between devices, extended(): lax.ppermute(head, axis, [((i + 1) % count, i) for i in range(ends)])  14.5 us
    dot_general x27, matrix products, convolve(): jnp.einsum('hwk,kc->hwc', window, piece[offset_y, offset_x], preferred_el...  11.5 us
    ppermute x6, starting transfers between devices, extended(): lax.ppermute(tail, axis, [(i, (i + 1) % count) for i in range(ends)])  8.66 us
    ppermute x6, waiting for transfers between devices, extended(): lax.ppermute(head, axis, [((i + 1) % count, i) for i in range(ends)])  8.53 us
    reshape x2, local copies, waits for them, and re-layouts, convolve(): piece = jnp.concatenate(lax.all_gather(own, ('row', 'col')), axis=2)  5.47 us
    all_gather x1, local copies, waits for them, and re-layouts, convolve(): piece = jnp.concatenate(lax.all_gather(own, ('row', 'col')), axis=2)  5.42 us
  transfers between devices with their start and end apart: 15, of which 7 were waited for; matrix products, arithmetic and copies ran while one was open for 11% of the time, Pallas kernels for 0%

profile of v1, /device:TPU:1, one launch (start us, length us, event | category | flops | bytes accessed | tf_op | source)
XLA Modules:
  0.0 218.6 jit_solution(13874784099330051905)
XLA Ops:
  8.4 1.7 constant_dynamic-slice_fusion.1
  10.2 1.7 constant_dynamic-slice_fusion
  13.2 31.2 %all-reduce.1 = (f32[32]{0:T(128)S(1)}, f32[32]{0:T(128)S(1)}) all-reduce(f32[32]{0:T(128)S(1)} %reduce_sum.54, f32[32]{0:T(128)S(1)} %reduce_sum.51), channel_id=1, replica_groups=mesh['img'=2,'row'=8,'col'=2] {'row','col'}, use_global_device_ids=true, to_apply=%region_5.6 | all-reduce | flops 64 | bytes 512 | tf_op jit(solution)/shard_map/psum | solution.py:32
  45.7 1.3 collective-permute-start
  48.3 1.8 collective-permute-done
  50.1 3.9 %collective-permute-done.1 = bf16[1,64,512]{2,1,0:T(8,128)(2,1)S(1)} collective-permute-done((bf16[1,64,512]{2,1,0:T(8,128)(2,1)S(1)}, bf16[1,64,512]{2,1,0:T(8,128)(2,1)S(1)}, u32[]{:S(2)}, u32[]{:S(2)}) %collective-permute-start.1) | collective-permute-done | bytes 65568 | tf_op jit(solution)/shard_map/ppermute | solution.py:20
  53.9 5.5 %collective-permute-start.3 = (bf16[3,1,512]{2,1,0:T(2,128)(2,1)S(1)}, bf16[3,1,512]{2,1,0:T(2,128)(2,1)S(1)}, u32[]{:S(2)}, u32[]{:S(2)}) collective-permute-start(bf16[3,1,512]{2,1,0:T(2,128)(2,1)S(1)} %get-tuple-element.20), channel_id=1, source_target_pairs={{1,0},{3,2},{5,4},{7,6},{9,8},{11,10},{13,12},{15,14},{17,16},{19,... | collective-permute-start | bytes 9224 | tf_op jit(solution)/shard_map/ppermute | solution.py:20
  60.7 7.5 %all-gather.7.cloned.1.call-done = bf16[48,3,32,512]{3,2,1,0:T(8,128)(2,1)} async-done(((bf16[3,3,32,512]{3,2,1,0:T(8,128)(2,1)}), bf16[48,3,32,512]{3,2,1,0:T(8,128)(2,1)}) %all-gather.7.cloned.1.call-update) | async-done | bytes 4718608 | tf_op jit(solution)/shard_map/all_gather | solution.py:52
  68.2 2.7 %copy.17 = bf16[3,3,16,32,512]{4,3,2,1,0:T(8,128)(2,1)S(1)} copy(bf16[3,3,16,32,512]{4,3,1,0,2:T(8,128)(2,1)} %bitcast.210) | data formatting | bytes 9437184 | tf_op jit(solution)/shard_map/reshape | solution.py:52
  73.4 29.7 %all-reduce = (f32[32]{0:T(128)S(1)}, f32[32]{0:T(128)S(1)}) all-reduce(f32[32]{0:T(128)S(1)} %reduce_sum.75, f32[32]{0:T(128)S(1)} %reduce_sum.72), channel_id=1, replica_groups=mesh['img'=2,'row'=8,'col'=2] {'row','col'}, use_global_device_ids=true, to_apply=%region_11.12 | all-reduce | flops 64 | bytes 512 | tf_op jit(solution)/shard_map/psum | solution.py:32
  106.0 19.2 %all-gather.9.cloned.1.call-done = bf16[48,3,32,512]{3,2,1,0:T(8,128)(2,1)} async-done(((bf16[3,3,32,512]{3,2,1,0:T(8,128)(2,1)}), bf16[48,3,32,512]{3,2,1,0:T(8,128)(2,1)}) %all-gather.9.cloned.1.call-update) | async-done | bytes 4718608 | tf_op jit(solution)/shard_map/all_gather | solution.py:52
  125.2 2.7 %copy.18 = bf16[3,3,16,32,512]{4,3,2,1,0:T(8,128)(2,1)S(1)} copy(bf16[3,3,16,32,512]{4,3,1,0,2:T(8,128)(2,1)} %bitcast.208) | data formatting | bytes 9437184 | tf_op jit(solution)/shard_map/reshape | solution.py:52
  127.9 2.2 copy-done.1
  130.3 48.9 %all-gather.11.cloned.1.call-done = bf16[48,3,32,512]{3,2,1,0:T(8,128)(2,1)} async-done(((bf16[3,3,32,512]{3,2,1,0:T(8,128)(2,1)}), bf16[48,3,32,512]{3,2,1,0:T(8,128)(2,1)}) %all-gather.11.cloned.1.call-update) | async-done | bytes 4718608 | tf_op jit(solution)/shard_map/all_gather | solution.py:52
  179.2 5.4 %copy.19 = bf16[16,3,3,32,512]{4,3,0,2,1:T(8,128)(2,1)} copy(bf16[16,3,3,32,512]{4,3,2,1,0:T(8,128)(2,1)} %bitcast.209) | data formatting | bytes 9437184 | tf_op jit(solution)/shard_map/all_gather | solution.py:52
  184.6 2.2 collective-permute-start.7
  188.5 1.3 collective-permute-done.6
  191.4 2.2 %collective-permute-start.8 = (bf16[1,128,512]{2,1,0:T(8,128)(2,1)S(1)}, bf16[1,128,512]{2,1,0:T(8,128)(2,1)S(1)}, u32[]{:S(2)}, u32[]{:S(2)}) collective-permute-start(bf16[1,128,512]{2,1,0:T(8,128)(2,1)S(1)} %slice.150), channel_id=1, source_target_pairs={{0,2},{2,4},{4,6},{6,8},{8,10},{10,12},{12,14},{1,3},{3,5},{5,7},{... | collective-permute-start | bytes 393224 | tf_op jit(solution)/shard_map/ppermute | solution.py:18
  194.9 1.5 fusion.31
  196.4 4.6 %collective-permute-done.9 = bf16[1,128,512]{2,1,0:T(8,128)(2,1)S(1)} collective-permute-done((bf16[1,128,512]{2,1,0:T(8,128)(2,1)S(1)}, bf16[1,128,512]{2,1,0:T(8,128)(2,1)S(1)}, u32[]{:S(2)}, u32[]{:S(2)}) %collective-permute-start.9) | collective-permute-done | bytes 131104 | tf_op jit(solution)/shard_map/ppermute | solution.py:20
  202.4 3.0 %collective-permute-start.11 = (bf16[4,1,512]{2,1,0:T(2,128)(2,1)S(1)}, bf16[4,1,512]{2,1,0:T(2,128)(2,1)S(1)}, u32[]{:S(2)}, u32[]{:S(2)}) collective-permute-start(bf16[4,1,512]{2,1,0:T(2,128)(2,1)S(1)} %get-tuple-element.16), channel_id=1, source_target_pairs={{1,0},{3,2},{5,4},{7,6},{9,8},{11,10},{13,12},{15,14},{17,16},{19,... | collective-permute-start | bytes 12296 | tf_op jit(solution)/shard_map/ppermute | solution.py:20
  205.5 1.3 fusion.34
  206.8 1.3 fusion.29
  208.4 1.3 fusion.32
  (96 shorter events, 20.8 us)
Async XLA Ops:
  6.5 61.6 %all-gather.7.cloned.1.call-start = ((), (), s32[]{:S(2)}) async-start(), calls=%async_computation | async-start | bytes 5013504 | tf_op jit(solution)/shard_map/all_gather | solution.py:52
  8.4 116.8 %all-gather.9.cloned.1.call-start = ((), (), s32[]{:S(2)}) async-start(), calls=%async_computation.1 | async-start | bytes 5013504 | tf_op jit(solution)/shard_map/all_gather | solution.py:52
  10.2 169.0 %all-gather.11.cloned.1.call-start = ((), (), s32[]{:S(2)}) async-start(), calls=%async_computation.2 | async-start | bytes 5013504 | tf_op jit(solution)/shard_map/all_gather | solution.py:52
  45.7 4.4 %collective-permute-start = (bf16[1,64,512]{2,1,0:T(8,128)(2,1)S(1)}, bf16[1,64,512]{2,1,0:T(8,128)(2,1)S(1)}, u32[]{:S(2)}, u32[]{:S(2)}) collective-permute-start(bf16[1,64,512]{2,1,0:T(8,128)(2,1)S(1)} %fusion.69), channel_id=1, source_target_pairs={{0,2},{2,4},{4,6},{6,8},{8,10},{10,12},{12,14},{1,3},{3,5},{5,7},{... | collective-permute-start | bytes 196616 | tf_op jit(solution)/shard_map/ppermute | solution.py:18
  47.0 6.9 %collective-permute-start.1 = (bf16[1,64,512]{2,1,0:T(8,128)(2,1)S(1)}, bf16[1,64,512]{2,1,0:T(8,128)(2,1)S(1)}, u32[]{:S(2)}, u32[]{:S(2)}) collective-permute-start(bf16[1,64,512]{2,1,0:T(8,128)(2,1)S(1)} %fusion.69), channel_id=1, source_target_pairs={{2,0},{4,2},{6,4},{8,6},{10,8},{12,10},{14,12},{3,1},{5,3},{7,5},{... | collective-permute-start | bytes 196616 | tf_op jit(solution)/shard_map/ppermute | solution.py:20
  53.9 17.0 %collective-permute-start.3 = (bf16[3,1,512]{2,1,0:T(2,128)(2,1)S(1)}, bf16[3,1,512]{2,1,0:T(2,128)(2,1)S(1)}, u32[]{:S(2)}, u32[]{:S(2)}) collective-permute-start(bf16[3,1,512]{2,1,0:T(2,128)(2,1)S(1)} %get-tuple-element.20), channel_id=1, source_target_pairs={{1,0},{3,2},{5,4},{7,6},{9,8},{11,10},{13,12},{15,14},{17,16},{19,... | collective-permute-start | bytes 9224 | tf_op jit(solution)/shard_map/ppermute | solution.py:20
  59.4 12.0 %collective-permute-start.2 = (bf16[3,1,512]{2,1,0:T(2,128)(2,1)S(1)}, bf16[3,1,512]{2,1,0:T(2,128)(2,1)S(1)}, u32[]{:S(2)}, u32[]{:S(2)}) collective-permute-start(bf16[3,1,512]{2,1,0:T(2,128)(2,1)S(1)} %get-tuple-element.19), channel_id=1, source_target_pairs={{0,1},{2,3},{4,5},{6,7},{8,9},{10,11},{12,13},{14,15},{16,17},{18,... | collective-permute-start | bytes 9224 | tf_op jit(solution)/shard_map/ppermute | solution.py:18
  70.9 32.4 %copy-start.5 = (f32[512]{0:T(512)S(1)}, f32[512]{0:T(512)}, u32[]{:S(2)}) copy-start(f32[512]{0:T(512)} %param.17) | copy-start | bytes 6148
  70.9 32.4 %copy-start.6 = (f32[512]{0:T(512)S(1)}, f32[512]{0:T(512)}, u32[]{:S(2)}) copy-start(f32[512]{0:T(512)} %param.16) | copy-start | bytes 6148
  103.4 81.2 %collective-permute-start.4 = (bf16[1,64,512]{2,1,0:T(8,128)(2,1)S(1)}, bf16[1,64,512]{2,1,0:T(8,128)(2,1)S(1)}, u32[]{:S(2)}, u32[]{:S(2)}) collective-permute-start(bf16[1,64,512]{2,1,0:T(8,128)(2,1)S(1)} %fusion.153), channel_id=1, source_target_pairs={{0,2},{2,4},{4,6},{6,8},{8,10},{10,12},{12,14},{1,3},{3,5},{5,7},{... | collective-permute-start | bytes 196616 | tf_op jit(solution)/shard_map/ppermute | solution.py:18
  104.7 79.9 %collective-permute-start.5 = (bf16[1,64,512]{2,1,0:T(8,128)(2,1)S(1)}, bf16[1,64,512]{2,1,0:T(8,128)(2,1)S(1)}, u32[]{:S(2)}, u32[]{:S(2)}) collective-permute-start(bf16[1,64,512]{2,1,0:T(8,128)(2,1)S(1)} %fusion.153), channel_id=1, source_target_pairs={{2,0},{4,2},{6,4},{8,6},{10,8},{12,10},{14,12},{3,1},{5,3},{7,5},{... | collective-permute-start | bytes 196616 | tf_op jit(solution)/shard_map/ppermute | solution.py:20
  127.9 2.2 %copy-start.1 = (bf16[3,3,16,32,512]{4,3,2,1,0:T(8,128)(2,1)}, bf16[3,3,16,32,512]{4,3,2,1,0:T(8,128)(2,1)S(1)}, u32[]{:S(2)}) copy-start(bf16[3,3,16,32,512]{4,3,2,1,0:T(8,128)(2,1)S(1)} %copy.18) | copy-start | bytes 14155780
  179.2 8.9 %copy-start.2 = (bf16[3,3,16,32,512]{4,3,2,1,0:T(8,128)(2,1)S(1)}, bf16[3,3,16,32,512]{4,3,2,1,0:T(8,128)(2,1)}, u32[]{:S(2)}) copy-start(bf16[3,3,16,32,512]{4,3,2,1,0:T(8,128)(2,1)} %copy-done.1) | copy-start | bytes 14155780
  184.6 6.4 %copy-start.3 = (bf16[1,64,512]{2,1,0:T(8,128)(2,1)S(1)}, bf16[1,64,512]{2,1,0:T(8,128)(2,1)}, u32[]{:S(2)}) copy-start(bf16[1,64,512]{2,1,0:T(8,128)(2,1)} %param.11) | copy-start | bytes 196612
  184.6 6.4 %copy-start.7 = (f32[512]{0:T(512)S(1)}, f32[512]{0:T(512)}, u32[]{:S(2)}) copy-start(f32[512]{0:T(512)} %param.19) | copy-start | bytes 6148
  184.6 5.7 %collective-permute-start.7 = (bf16[3,1,512]{2,1,0:T(2,128)(2,1)S(1)}, bf16[3,1,512]{2,1,0:T(2,128)(2,1)S(1)}, u32[]{:S(2)}, u32[]{:S(2)}) collective-permute-start(bf16[3,1,512]{2,1,0:T(2,128)(2,1)S(1)} %get-tuple-element.18), channel_id=1, source_target_pairs={{1,0},{3,2},{5,4},{7,6},{9,8},{11,10},{13,12},{15,14},{17,16},{19,... | collective-permute-start | bytes 9224 | tf_op jit(solution)/shard_map/ppermute | solution.py:20
  186.8 3.1 %collective-permute-start.6 = (bf16[3,1,512]{2,1,0:T(2,128)(2,1)S(1)}, bf16[3,1,512]{2,1,0:T(2,128)(2,1)S(1)}, u32[]{:S(2)}, u32[]{:S(2)}) collective-permute-start(bf16[3,1,512]{2,1,0:T(2,128)(2,1)S(1)} %get-tuple-element.17), channel_id=1, source_target_pairs={{0,1},{2,3},{4,5},{6,7},{8,9},{10,11},{12,13},{14,15},{16,17},{18,... | collective-permute-start | bytes 9224 | tf_op jit(solution)/shard_map/ppermute | solution.py:18
  190.1 19.6 %slice-start = ((s8[4718592]{0:T(1024)(128)(4,1)}), s8[524288]{0:T(1024)(128)(4,1)S(1)}, s32[]{:S(2)}) async-start(s8[4718592]{0:T(1024)(128)(4,1)} %bitcast.201), calls=%async_computation.3 | async-start | bytes 1048576
  191.4 5.0 %collective-permute-start.8 = (bf16[1,128,512]{2,1,0:T(8,128)(2,1)S(1)}, bf16[1,128,512]{2,1,0:T(8,128)(2,1)S(1)}, u32[]{:S(2)}, u32[]{:S(2)}) collective-permute-start(bf16[1,128,512]{2,1,0:T(8,128)(2,1)S(1)} %slice.150), channel_id=1, source_target_pairs={{0,2},{2,4},{4,6},{6,8},{8,10},{10,12},{12,14},{1,3},{3,5},{5,7},{... | collective-permute-start | bytes 393224 | tf_op jit(solution)/shard_map/ppermute | solution.py:18
  193.6 7.5 %collective-permute-start.9 = (bf16[1,128,512]{2,1,0:T(8,128)(2,1)S(1)}, bf16[1,128,512]{2,1,0:T(8,128)(2,1)S(1)}, u32[]{:S(2)}, u32[]{:S(2)}) collective-permute-start(bf16[1,128,512]{2,1,0:T(8,128)(2,1)S(1)} %slice.150), channel_id=1, source_target_pairs={{2,0},{4,2},{6,4},{8,6},{10,8},{12,10},{14,12},{3,1},{5,3},{7,5},{... | collective-permute-start | bytes 393224 | tf_op jit(solution)/shard_map/ppermute | solution.py:20
  194.9 14.8 %slice-start.1 = ((s8[4718592]{0:T(1024)(128)(4,1)}), s8[4194304]{0:T(1024)(128)(4,1)S(1)}, s32[]{:S(2)}) async-start(s8[4718592]{0:T(1024)(128)(4,1)} %bitcast.201), calls=%async_computation.4 | async-start | bytes 8388608
  201.1 7.0 %collective-permute-start.10 = (bf16[4,1,512]{2,1,0:T(2,128)(2,1)S(1)}, bf16[4,1,512]{2,1,0:T(2,128)(2,1)S(1)}, u32[]{:S(2)}, u32[]{:S(2)}) collective-permute-start(bf16[4,1,512]{2,1,0:T(2,128)(2,1)S(1)} %get-tuple-element.15), channel_id=1, source_target_pairs={{0,1},{2,3},{4,5},{6,7},{8,9},{10,11},{12,13},{14,15},{16,17},{18,... | collective-permute-start | bytes 12296 | tf_op jit(solution)/shard_map/ppermute | solution.py:18
  202.4 5.7 %collective-permute-start.11 = (bf16[4,1,512]{2,1,0:T(2,128)(2,1)S(1)}, bf16[4,1,512]{2,1,0:T(2,128)(2,1)S(1)}, u32[]{:S(2)}, u32[]{:S(2)}) collective-permute-start(bf16[4,1,512]{2,1,0:T(2,128)(2,1)S(1)} %get-tuple-element.16), channel_id=1, source_target_pairs={{1,0},{3,2},{5,4},{7,6},{9,8},{11,10},{13,12},{15,14},{17,16},{19,... | collective-permute-start | bytes 12296 | tf_op jit(solution)/shard_map/ppermute | solution.py:20
  208.3 2.6 %copy-start.8 = (f32[512]{0:T(512)S(1)}, f32[512]{0:T(512)}, u32[]{:S(2)}) copy-start(f32[512]{0:T(512)} %param.21) | copy-start | bytes 6148
  (2 other events, 2.8 us)
Sparse Core Ops, SparseCore 0:
  9.6 58.5 all-gather.6
  70.5 54.6 all-gather.8
  127.5 51.6 all-gather.10
